TPU v7x, 32 devices: a whole 2x2x4 slice. The times are simulated.
32 devices in a mesh: outer: 8 (over z, x), inner: 4 (over y, core).
Axes of the slice: x: 2, y: 2, z: 4, core: 2. Of those that a mesh axis runs over, the one named last changes fastest.
Arguments:
- queries: bfloat16 [8192, 1024], P(('outer', 'inner')), may hold values from -10 to 10
- keys: bfloat16 [8192, 256], P(('outer', 'inner')), may hold values from -10 to 10
- values: bfloat16 [8192, 256], P(('outer', 'inner')), may hold values from -18 to 18
- pool_fine: float32 [16, 8], replicated, may hold values from -1.5 to 1.5
- pool_coarse: float32 [8, 8], replicated, may hold values from -2 to 2
- gain: float32 [1024], replicated, may hold values from 0.5 to 1.5
Outputs:
- normed: bfloat16 [8192, 1024], P(('outer', 'inner'))
All inputs are finite; a program needn't handle non-finite values.
Results may differ from a plain program's by a relative error of at most 0.008.
Values may be sent and summed in bfloat16 or wider, within the bound.
A program may use at most 64 MiB of HBM per device.

v0:
```python
import jax
import jax.numpy as jnp
from jax import lax
from jax.sharding import PartitionSpec as P

HQ = 16
KVH = 4
HD = 64
BLOCK = 512
FINE = 16
RATIO = 8
COARSE = 128


EPSILON = 1e-06
MASKED_SCORE = -1e30


def shifted(value, axis, steps):
    count = lax.axis_size(axis)
    first, last = (max(0, -steps), min(count, count - steps))
    return lax.ppermute(value, axis, [(source, source + steps) for source in range(first, last)])


def summarize(source, pooling, factor):
    amount = source.shape[0] // factor
    shaped = source.astype(jnp.float32).reshape(amount, factor, 2, KVH, HD)
    weights = pooling.reshape(factor, 2, KVH)
    pooled = jnp.einsum("mjskd,jsk->mskd", shaped, weights, precision=lax.Precision.HIGHEST)
    return pooled.reshape(amount, 2 * KVH * HD).astype(jnp.bfloat16)


def partial_state(stacked, keyset, allowed):
    amount = keyset.shape[0]
    kv_width = KVH * HD
    group_size = HQ // KVH
    tok_rows = allowed.shape[0]
    key_heads = keyset[:, :kv_width].reshape(amount, KVH, HD).transpose(1, 0, 2)
    value_heads = keyset[:, kv_width:].reshape(amount, KVH, HD).transpose(1, 0, 2)

    def one_group(group_idx):
        query_rows = lax.dynamic_index_in_dim(stacked, group_idx, 0, False)
        key_head = lax.dynamic_index_in_dim(key_heads, group_idx, 0, False)
        value_head = lax.dynamic_index_in_dim(value_heads, group_idx, 0, False)
        scores = lax.dot_general(
            query_rows, key_head, (((1,), (1,)), ((), ())), preferred_element_type=jnp.float32
        )
        scores = scores.reshape(group_size, tok_rows, amount)
        scores = jnp.where(allowed[None], scores * HD ** (-0.5), MASKED_SCORE)
        peak = jnp.max(scores, axis=2)
        expon = jnp.where(allowed[None], jnp.exp(scores - peak[..., None]), 0.0)
        totals = jnp.sum(expon, axis=2)
        weights = expon.astype(jnp.bfloat16).reshape(group_size * tok_rows, amount)
        blended = jnp.dot(weights, value_head, preferred_element_type=jnp.float32)
        return (peak.reshape(group_size * tok_rows), totals.reshape(group_size * tok_rows), blended)

    return lax.map(one_group, jnp.arange(KVH))


def merge_states(former, latter):
    peak = jnp.maximum(former[0], latter[0])
    leading = jnp.exp(former[0] - peak)
    trailing = jnp.exp(latter[0] - peak)
    totals = former[1] * leading + latter[1] * trailing
    blended = former[2] * leading[..., None] + latter[2] * trailing[..., None]
    return (peak, totals, blended)


def local(queries, keys, values, pool_fine, pool_coarse, gain):
    tok_dev = queries.shape[0]
    group_size = HQ // KVH
    inner_count = lax.axis_size("inner")
    devices_all = lax.axis_size("outer") * inner_count
    device = lax.axis_index(("outer", "inner"))
    group_index = lax.axis_index("outer")
    dev_start = device * tok_dev
    group_tok = tok_dev * inner_count
    query_block = (dev_start + jnp.arange(tok_dev)) // BLOCK
    stacked = (
        queries.reshape(tok_dev, KVH, group_size, HD)
        .transpose(1, 2, 0, 3)
        .reshape(KVH, group_size * tok_dev, HD)
    )
    paired = jnp.concatenate([keys, values], axis=1)
    reach = max(1, 2 * BLOCK // tok_dev - 1)
    offsets = list(range(reach, 0, -1)) + list(range(-1, -reach - 1, -1))
    shifted_parts = []
    for offset in offsets:
        shifted_parts.append(shifted(paired, ("outer", "inner"), offset))
    window = jnp.concatenate(shifted_parts[:reach] + [paired] + shifted_parts[reach:], axis=0)
    key_pos = dev_start - reach * tok_dev + jnp.arange(window.shape[0])
    inside = (key_pos >= 0) & (key_pos < devices_all * tok_dev)
    near_ok = inside[None, :] & (jnp.abs(key_pos[None, :] // BLOCK - query_block[:, None]) <= 1)
    merged = partial_state(stacked, window, near_ok)
    fine_local = summarize(paired, pool_fine, FINE)
    group_fine = lax.all_gather(fine_local, "inner", axis=0, tiled=True)
    fine_pos = group_index * group_tok + jnp.arange(group_fine.shape[0]) * FINE
    fine_ok = jnp.abs(fine_pos[None, :] // BLOCK - query_block[:, None]) > 1
    merged = merge_states(merged, partial_state(stacked, group_fine, fine_ok))
    coarse_group = summarize(group_fine, pool_coarse, RATIO)
    portion = lax.all_gather(coarse_group, "outer", axis=0, tiled=True)
    coarse_pos = jnp.arange(portion.shape[0]) * COARSE
    far_group = (coarse_pos // group_tok != group_index)[None, :]
    merged = merge_states(
        merged,
        partial_state(
            stacked,
            portion,
            far_group & (jnp.abs(coarse_pos[None, :] // BLOCK - query_block[:, None]) > 1),
        ),
    )
    attended = merged[2] / merged[1][..., None]
    attended = (
        attended.reshape(KVH, group_size, tok_dev, HD)
        .transpose(2, 0, 1, 3)
        .reshape(tok_dev, HQ * HD)
    )
    rescale = lax.rsqrt(jnp.mean(attended * attended, axis=1, keepdims=True) + EPSILON)
    return (attended * rescale * gain).astype(jnp.bfloat16)


def solution(mesh):
    placed = (
        P(("outer", "inner"), None),
        P(("outer", "inner"), None),
        P(("outer", "inner"), None),
        P(),
        P(),
        P(),
    )
    return jax.shard_map(
        local, mesh=mesh, in_specs=placed, out_specs=P(("outer", "inner"), None), check_vma=False
    )
```

profile of v0, /device:TPU:1, one launch (start us, length us, event | category | flops | bytes accessed | tf_op | source)
XLA Modules:
  0.0 155.6 jit_solution(796350974592890757)
XLA Ops:
  2.1 5.2 %collective-permute-start = (bf16[256,512]{0,1:T(8,128)(2,1)S(1)}, bf16[256,512]{0,1:T(8,128)(2,1)}, u32[]{:S(2)}, u32[]{:S(2)}) collective-permute-start(bf16[256,512]{0,1:T(8,128)(2,1)S(1)} %pad_maximum_fusion), channel_id=1, source_target_pairs={{0,3},{1,4},{2,5},{3,6},{4,7},{5,8},{6,9},{7,10},{8,11},{9,12},{10... | collective-permute-start | bytes 786440 | tf_op jit(solution)/shard_map/ppermute | solution.py:22
  7.3 3.2 %collective-permute-start.1 = (bf16[256,512]{0,1:T(8,128)(2,1)S(1)}, bf16[256,512]{0,1:T(8,128)(2,1)}, u32[]{:S(2)}, u32[]{:S(2)}) collective-permute-start(bf16[256,512]{0,1:T(8,128)(2,1)S(1)} %pad_maximum_fusion), channel_id=1, source_target_pairs={{0,2},{1,3},{2,4},{3,5},{4,6},{5,7},{6,8},{7,9},{8,10},{9,11},{10,... | collective-permute-start | bytes 786440 | tf_op jit(solution)/shard_map/ppermute | solution.py:22
  10.5 2.4 %collective-permute-start.2 = (bf16[256,512]{0,1:T(8,128)(2,1)S(1)}, bf16[256,512]{0,1:T(8,128)(2,1)}, u32[]{:S(2)}, u32[]{:S(2)}) collective-permute-start(bf16[256,512]{0,1:T(8,128)(2,1)S(1)} %pad_maximum_fusion), channel_id=1, source_target_pairs={{0,1},{1,2},{2,3},{3,4},{4,5},{5,6},{6,7},{7,8},{8,9},{9,10},{10,1... | collective-permute-start | bytes 786440 | tf_op jit(solution)/shard_map/ppermute | solution.py:22
  12.9 2.6 %collective-permute-start.3 = (bf16[256,512]{0,1:T(8,128)(2,1)S(1)}, bf16[256,512]{0,1:T(8,128)(2,1)}, u32[]{:S(2)}, u32[]{:S(2)}) collective-permute-start(bf16[256,512]{0,1:T(8,128)(2,1)S(1)} %pad_maximum_fusion), channel_id=1, source_target_pairs={{1,0},{2,1},{3,2},{4,3},{5,4},{6,5},{7,6},{8,7},{9,8},{10,9},{11,1... | collective-permute-start | bytes 786440 | tf_op jit(solution)/shard_map/ppermute | solution.py:22
  15.5 1.3 collective-permute-start.4
  17.7 10.2 %all_gather.6 = bf16[64,512]{1,0:T(8,128)(2,1)S(1)} all-gather(bf16[16,512]{1,0:T(8,128)(2,1)S(1)} %convert_element_type.34), channel_id=1, replica_groups=mesh['outer'=8,'inner'=4] {'inner'}, dimensions={0}, use_global_device_ids=true | all-gather | bytes 81920 | tf_op jit(solution)/shard_map/all_gather | solution.py:96
  29.1 30.7 %all_gather.7 = bf16[64,512]{1,0:T(8,128)(2,1)S(1)} all-gather(bf16[8,512]{1,0:T(8,128)(2,1)S(1)} %convert_element_type.37), channel_id=1, replica_groups=mesh['outer'=8,'inner'=4] {'outer'}, dimensions={0}, use_global_device_ids=true | all-gather | bytes 73728 | tf_op jit(solution)/shard_map/all_gather | solution.py:101
  60.2 12.8 %while.47 = (s32[]{:T(128)}, f32[4,1024]{1,0:T(4,128)S(1)}, f32[4,1024]{1,0:T(4,128)S(1)}, f32[4,1024,64]{1,2,0:T(8,128)S(1)}, s32[4]{0:T(128)S(1)}, /*index=5*/...) while((s32[]{:T(128)}, f32[4,1024]{1,0:T(4,128)S(1)}, ...), condition=%wide.region_11.12_spmd.clone, body=%wide.region_8.11_spmd.clone.sunk | while | flops 17299460 | bytes 2094603 | solution.py:57
  75.7 22.9 %while.46 = (s32[]{:T(128)}, f32[4,1024]{1,0:T(4,128)}, f32[4,1024]{1,0:T(4,128)}, f32[4,1024,64]{1,2,0:T(8,128)S(1)}, s32[4]{0:T(128)S(1)}, /*index=5*/bf16[4,1...) while((s32[]{:T(128)}, f32[4,1024]{1,0:T(4,128)}, ...), condition=%wide.region_7.8_spmd.clone, body=%wide.region_4.7_spmd.clone.sunk | while | flops 17283076 | bytes 2094531 | solution.py:57
  78.7 1.3 dynamic_update_slice.55
  80.1 1.4 dynamic_update_slice.54
  84.4 1.3 dynamic_update_slice.55
  85.8 1.4 dynamic_update_slice.54
  90.2 1.3 dynamic_update_slice.55
  91.5 1.4 dynamic_update_slice.54
  95.9 1.3 dynamic_update_slice.55
  97.2 1.4 dynamic_update_slice.54
  98.6 1.3 collective-permute-start.5
  104.8 8.0 %collective-permute-done.5 = bf16[256,512]{0,1:T(8,128)(2,1)S(1)} collective-permute-done((bf16[256,512]{0,1:T(8,128)(2,1)S(1)}, bf16[256,512]{0,1:T(8,128)(2,1)S(1)}, u32[]{:S(2)}, u32[]{:S(2)}) %collective-permute-start.5) | collective-permute-done | bytes 262176 | tf_op jit(solution)/shard_map/ppermute | solution.py:22
  114.1 37.0 %while.45 = (s32[]{:T(128)}, f32[4,1024]{1,0:T(4,128)S(1)}, f32[4,1024]{1,0:T(4,128)S(1)}, f32[4,1024,64]{1,2,0:T(8,128)S(1)}, s32[4]{0:T(128)S(1)}, /*index=5*/...) while((s32[]{:T(128)}, f32[4,1024]{1,0:T(4,128)S(1)}, ...), condition=%wide.region_3.4_spmd.clone, body=%wide.region_0.3_spmd.clone.sunk | while | flops 488110080 | bytes 24827852 | solution.py:57
  117.1 2.5 %fusion.94 = (f32[4,256]{1,0:T(4,128)S(1)}, f32[4,256,1792]{2,1,0:T(8,128)S(1)}) fusion(pred[256,1792]{1,0:T(8,128)(4,1)S(1)} %fusion.93, bf16[4,1792,64]{1,2,0:T(8,128)(2,1)} %get-tuple-element.724, s32[]{:T(128)S(6)} %select_n.146, bf16[4,256,64]{1,0,2:T(4,128)(2,1)S(1)} %dot_general.44), kind=kOutput, calls=%fused_computation.5.clone.1 | convolution fusion | flops 240385024 | bytes 8163332 | tf_op jit(solution)/shard_map/while/body/eval_jaxpr/dot_general | solution.py:45
  119.6 2.3 %fusion.95 = (bf16[4,256,1792]{2,1,0:T(8,128)(2,1)S(1)}, f32[4,256]{1,0:T(4,128)S(1)}) fusion(f32[4,256,1792]{2,1,0:T(8,128)S(1)} %get-tuple-element.577, f32[4,256]{1,0:T(4,128)S(1)} %get-tuple-element.576, pred[256,1792]{1,0:T(8,128)(4,1)S(1)} %fusion.93), kind=kLoop, calls=%fused_computation.6.clone.1 | loop fusion | flops 11009024 | bytes 11476992 | tf_op jit(solution)/shard_map/while/body/eval_jaxpr/convert_element_type | solution.py:53
  121.9 1.2 fusion.96
  126.4 2.5 %fusion.94 = (f32[4,256]{1,0:T(4,128)S(1)}, f32[4,256,1792]{2,1,0:T(8,128)S(1)}) fusion(pred[256,1792]{1,0:T(8,128)(4,1)S(1)} %fusion.93, bf16[4,1792,64]{1,2,0:T(8,128)(2,1)} %get-tuple-element.724, s32[]{:T(128)S(6)} %select_n.146, bf16[4,256,64]{1,0,2:T(4,128)(2,1)S(1)} %dot_general.44), kind=kOutput, calls=%fused_computation.5.clone.1 | convolution fusion | flops 240385024 | bytes 8163332 | tf_op jit(solution)/shard_map/while/body/eval_jaxpr/dot_general | solution.py:45
  128.9 2.3 %fusion.95 = (bf16[4,256,1792]{2,1,0:T(8,128)(2,1)S(1)}, f32[4,256]{1,0:T(4,128)S(1)}) fusion(f32[4,256,1792]{2,1,0:T(8,128)S(1)} %get-tuple-element.577, f32[4,256]{1,0:T(4,128)S(1)} %get-tuple-element.576, pred[256,1792]{1,0:T(8,128)(4,1)S(1)} %fusion.93), kind=kLoop, calls=%fused_computation.6.clone.1 | loop fusion | flops 11009024 | bytes 11476992 | tf_op jit(solution)/shard_map/while/body/eval_jaxpr/convert_element_type | solution.py:53
  131.2 1.2 fusion.96
  135.6 2.5 %fusion.94 = (f32[4,256]{1,0:T(4,128)S(1)}, f32[4,256,1792]{2,1,0:T(8,128)S(1)}) fusion(pred[256,1792]{1,0:T(8,128)(4,1)S(1)} %fusion.93, bf16[4,1792,64]{1,2,0:T(8,128)(2,1)} %get-tuple-element.724, s32[]{:T(128)S(6)} %select_n.146, bf16[4,256,64]{1,0,2:T(4,128)(2,1)S(1)} %dot_general.44), kind=kOutput, calls=%fused_computation.5.clone.1 | convolution fusion | flops 240385024 | bytes 8163332 | tf_op jit(solution)/shard_map/while/body/eval_jaxpr/dot_general | solution.py:45
  138.1 2.3 %fusion.95 = (bf16[4,256,1792]{2,1,0:T(8,128)(2,1)S(1)}, f32[4,256]{1,0:T(4,128)S(1)}) fusion(f32[4,256,1792]{2,1,0:T(8,128)S(1)} %get-tuple-element.577, f32[4,256]{1,0:T(4,128)S(1)} %get-tuple-element.576, pred[256,1792]{1,0:T(8,128)(4,1)S(1)} %fusion.93), kind=kLoop, calls=%fused_computation.6.clone.1 | loop fusion | flops 11009024 | bytes 11476992 | tf_op jit(solution)/shard_map/while/body/eval_jaxpr/convert_element_type | solution.py:53
  140.4 1.2 fusion.96
  144.9 2.5 %fusion.94 = (f32[4,256]{1,0:T(4,128)S(1)}, f32[4,256,1792]{2,1,0:T(8,128)S(1)}) fusion(pred[256,1792]{1,0:T(8,128)(4,1)S(1)} %fusion.93, bf16[4,1792,64]{1,2,0:T(8,128)(2,1)} %get-tuple-element.724, s32[]{:T(128)S(6)} %select_n.146, bf16[4,256,64]{1,0,2:T(4,128)(2,1)S(1)} %dot_general.44), kind=kOutput, calls=%fused_computation.5.clone.1 | convolution fusion | flops 240385024 | bytes 8163332 | tf_op jit(solution)/shard_map/while/body/eval_jaxpr/dot_general | solution.py:45
  147.4 2.3 %fusion.95 = (bf16[4,256,1792]{2,1,0:T(8,128)(2,1)S(1)}, f32[4,256]{1,0:T(4,128)S(1)}) fusion(f32[4,256,1792]{2,1,0:T(8,128)S(1)} %get-tuple-element.577, f32[4,256]{1,0:T(4,128)S(1)} %get-tuple-element.576, pred[256,1792]{1,0:T(8,128)(4,1)S(1)} %fusion.93), kind=kLoop, calls=%fused_computation.6.clone.1 | loop fusion | flops 11009024 | bytes 11476992 | tf_op jit(solution)/shard_map/while/body/eval_jaxpr/convert_element_type | solution.py:53
  151.2 2.0 %add_divide_fusion = f32[4,1024,64]{1,2,0:T(8,128)S(1)} fusion(f32[4,1024,64]{1,2,0:T(8,128)} %copy-done.1, f32[4,1024,64]{1,2,0:T(8,128)} %copy-done.2, f32[4,1024,64]{1,2,0:T(8,128)S(1)} %get-tuple-element.152, f32[4,1024]{1,0:T(4,128)S(1)} %get-tuple-element.367, f32[4,1024]{1,0:T(4,128)S(1)} %get-tuple-element.371, f32[4,1024]{1,0:T(4,128)S(1)} %get-tuple-element.370, ...), kind=kLoop, calls=%fused_computation.60 | loop fusion | flops 1835008 | bytes 4276224 | tf_op jit(solution)/shard_map/div | solution.py:112
  (208 shorter events, 33.3 us)
Async XLA Ops:
  0.0 17.2 %copy-start = (f32[16,8]{0,1:T(8,128)S(1)}, f32[16,8]{0,1:T(8,128)}, u32[]{:S(2)}) copy-start(f32[16,8]{0,1:T(8,128)} %param.15) | copy-start | bytes 1540
  0.0 28.1 %copy-start.3 = (bf16[256,1024]{1,0:T(8,128)(2,1)S(1)}, bf16[256,1024]{1,0:T(8,128)(2,1)}, u32[]{:S(2)}) copy-start(bf16[256,1024]{1,0:T(8,128)(2,1)} %param.12) | copy-start | bytes 1572868
  2.1 96.5 %collective-permute-start = (bf16[256,512]{0,1:T(8,128)(2,1)S(1)}, bf16[256,512]{0,1:T(8,128)(2,1)}, u32[]{:S(2)}, u32[]{:S(2)}) collective-permute-start(bf16[256,512]{0,1:T(8,128)(2,1)S(1)} %pad_maximum_fusion), channel_id=1, source_target_pairs={{0,3},{1,4},{2,5},{3,6},{4,7},{5,8},{6,9},{7,10},{8,11},{9,12},{10... | collective-permute-start | bytes 786440 | tf_op jit(solution)/shard_map/ppermute | solution.py:22
  7.3 93.6 %collective-permute-start.1 = (bf16[256,512]{0,1:T(8,128)(2,1)S(1)}, bf16[256,512]{0,1:T(8,128)(2,1)}, u32[]{:S(2)}, u32[]{:S(2)}) collective-permute-start(bf16[256,512]{0,1:T(8,128)(2,1)S(1)} %pad_maximum_fusion), channel_id=1, source_target_pairs={{0,2},{1,3},{2,4},{3,5},{4,6},{5,7},{6,8},{7,9},{8,10},{9,11},{10,... | collective-permute-start | bytes 786440 | tf_op jit(solution)/shard_map/ppermute | solution.py:22
  10.5 91.4 %collective-permute-start.2 = (bf16[256,512]{0,1:T(8,128)(2,1)S(1)}, bf16[256,512]{0,1:T(8,128)(2,1)}, u32[]{:S(2)}, u32[]{:S(2)}) collective-permute-start(bf16[256,512]{0,1:T(8,128)(2,1)S(1)} %pad_maximum_fusion), channel_id=1, source_target_pairs={{0,1},{1,2},{2,3},{3,4},{4,5},{5,6},{6,7},{7,8},{8,9},{9,10},{10,1... | collective-permute-start | bytes 786440 | tf_op jit(solution)/shard_map/ppermute | solution.py:22
  12.9 90.0 %collective-permute-start.3 = (bf16[256,512]{0,1:T(8,128)(2,1)S(1)}, bf16[256,512]{0,1:T(8,128)(2,1)}, u32[]{:S(2)}, u32[]{:S(2)}) collective-permute-start(bf16[256,512]{0,1:T(8,128)(2,1)S(1)} %pad_maximum_fusion), channel_id=1, source_target_pairs={{1,0},{2,1},{3,2},{4,3},{5,4},{6,5},{7,6},{8,7},{9,8},{10,9},{11,1... | collective-permute-start | bytes 786440 | tf_op jit(solution)/shard_map/ppermute | solution.py:22
  15.5 88.4 %collective-permute-start.4 = (bf16[256,512]{0,1:T(8,128)(2,1)S(1)}, bf16[256,512]{0,1:T(8,128)(2,1)}, u32[]{:S(2)}, u32[]{:S(2)}) collective-permute-start(bf16[256,512]{0,1:T(8,128)(2,1)S(1)} %pad_maximum_fusion), channel_id=1, source_target_pairs={{2,0},{3,1},{4,2},{5,3},{6,4},{7,5},{8,6},{9,7},{10,8},{11,9},{12,... | collective-permute-start | bytes 786440 | tf_op jit(solution)/shard_map/ppermute | solution.py:22
  17.2 11.4 %copy-start.11 = (f32[8,8]{1,0:T(8,128)S(1)}, f32[8,8]{1,0:T(8,128)}, u32[]{:S(2)}) copy-start(f32[8,8]{1,0:T(8,128)} %param.16) | copy-start | bytes 772
  73.0 0.6 copy-start.4
  73.6 0.6 copy-start.6
  74.2 1.5 copy-start.1
  98.6 14.2 %copy-start.2 = (f32[4,1024,64]{1,2,0:T(8,128)}, f32[4,1024,64]{1,2,0:T(8,128)S(1)}, u32[]{:S(2)}) copy-start(f32[4,1024,64]{1,2,0:T(8,128)S(1)} %get-tuple-element.155) | copy-start | bytes 3145732
  98.6 14.2 %collective-permute-start.5 = (bf16[256,512]{0,1:T(8,128)(2,1)S(1)}, bf16[256,512]{0,1:T(8,128)(2,1)S(1)}, u32[]{:S(2)}, u32[]{:S(2)}) collective-permute-start(bf16[256,512]{0,1:T(8,128)(2,1)S(1)} %pad_maximum_fusion), channel_id=1, source_target_pairs={{3,0},{4,1},{5,2},{6,3},{7,4},{8,5},{9,6},{10,7},{11,8},{12,9},{13... | collective-permute-start | bytes 786440 | tf_op jit(solution)/shard_map/ppermute | solution.py:22
  114.0 37.1 %copy-start.5 = (f32[4,1024]{1,0:T(4,128)S(1)}, f32[4,1024]{1,0:T(4,128)}, u32[]{:S(2)}) copy-start(f32[4,1024]{1,0:T(4,128)} %copy-done.4) | copy-start | bytes 49156
  114.0 37.1 %copy-start.7 = (f32[4,1024]{1,0:T(4,128)S(1)}, f32[4,1024]{1,0:T(4,128)}, u32[]{:S(2)}) copy-start(f32[4,1024]{1,0:T(4,128)} %copy-done.6) | copy-start | bytes 49156
  114.1 37.1 %copy-start.8 = (f32[4,1024]{1,0:T(4,128)S(1)}, f32[4,1024]{1,0:T(4,128)}, u32[]{:S(2)}) copy-start(f32[4,1024]{1,0:T(4,128)} %get-tuple-element.154) | copy-start | bytes 49156
  114.1 37.1 %copy-start.9 = (f32[4,1024]{1,0:T(4,128)S(1)}, f32[4,1024]{1,0:T(4,128)}, u32[]{:S(2)}) copy-start(f32[4,1024]{1,0:T(4,128)} %get-tuple-element.159) | copy-start | bytes 49156
  153.7 0.7 copy-start.10
where the time goes:
time: 157 us; the launch traced here: 156 us
  blocking collectives  40.9 us (26%)
  local copies, waits for them, and re-layouts  34.6 us (22%)
  loops' own time  21.4 us (14%)
  matrix products  18.7 us (12%)
  starting transfers between devices  15.9 us (10%)
  other arithmetic  15.6 us (10%)
  waiting for transfers between devices  7.96 us (5%)
    all_gather x1, blocking collectives, local(): portion = lax.all_gather(coarse_group, 'outer', axis=0, tiled=True)  30.7 us
    another operation x3, loops' own time, partial_state(): return lax.map(one_group, jnp.arange(KVH))  21.4 us
    ppermute x6, starting transfers between devices, shifted(): lax.ppermute(value, axis, [(source, source + steps) for source in range(f...  15.9 us
    dynamic_update_slice x24, local copies, waits for them, and re-layouts, partial_state(): return lax.map(one_group, jnp.arange(KVH))  12 us
    dot_general x12, matrix products, one_group(): lax.dot_general(query_rows, key_head, (((1,), (1,)), ((), ())), preferred...  11.4 us
    all_gather x1, blocking collectives, local(): group_fine = lax.all_gather(fine_local, 'inner', axis=0, tiled=True)  10.2 us
    convert_element_type x4, other arithmetic, one_group(): weights = expon.astype(jnp.bfloat16).reshape(group_size * tok_rows, amount)  9.25 us
    unnamed x37, local copies, waits for them, and re-layouts  8.63 us
  transfers between devices with their start and end apart: 6, of which 1 were waited for; matrix products, arithmetic and copies ran while one was open for 19% of the time, Pallas kernels for 0%

commit v1 on v0

v1 whole, which is shorter than its diff:
```python
import functools
import math

import jax
import jax.numpy as jnp
from jax import lax
from jax.experimental import pallas as pl
from jax.experimental.pallas import tpu as pltpu
from jax.sharding import PartitionSpec as P

HQ = 16
KVH = 4
HD = 64
BLOCK = 512
FINE = 16
RATIO = 8
COARSE = 128

EPSILON = 1e-06
MASKED_SCORE = -1e30
LANES = 128
MESH = pl.DeviceIdType.MESH
BF16 = jnp.bfloat16
F32 = jnp.float32


def kernel(
    outer_count, inner_count,
    q_ref, k_ref, v_ref, pf_ref, pc_ref, gain_ref, out_ref,
    q_all, own_k, own_v, mate_k, mate_v, other_k, other_v,
    ka, va, kb, vb, kc, vc, bias_ref,
    fine_send, fine_all, coarse_send, coarse_pad, coarse_group, coarse_all,
    peaks, sums, att_own, att_send, att_recv,
    q_ss, q_rs, own_ss, own_rs, mate_ss, mate_rs, other_ss, other_rs,
    fine_ss, fine_rs, cg_ss, cg_rs, co_ss, co_rs, att_ss, att_rs,
):
    tok = q_ref.shape[0]
    ranks = BLOCK // tok
    kv_width = KVH * HD
    share = kv_width // ranks
    q_share = HQ * HD // ranks
    tiles = q_share // LANES
    kv_local = share // HD
    tiles_per_kv = tiles // kv_local
    fine_dev = tok // FINE
    coarse_dev = tok // COARSE
    group_tok = tok * inner_count
    fine_amount = group_tok // FINE
    coarse_amount = outer_count * group_tok // COARSE
    blocks = outer_count * inner_count // ranks
    factor = HD ** (-0.5) * math.log2(math.e)

    o_me = lax.axis_index("outer")
    i_me = lax.axis_index("inner")
    linear = o_me * inner_count + i_me
    block = linear // ranks
    rank = lax.rem(linear, ranks)
    odd = lax.rem(block, 2)
    mate = block + 1 - 2 * odd
    other = block - 1 + 2 * odd
    has_other = (other >= 0) & (other < blocks)

    def at_rank(which_block, rel):
        target_rank = lax.rem(rank + rel, ranks)
        spot = which_block * ranks + target_rank
        return (spot // inner_count, lax.rem(spot, inner_count)), target_rank

    inner_peers = [lax.rem(i_me + rel, inner_count) for rel in range(1, inner_count)]
    outer_peers = [lax.rem(o_me + rel, outer_count) for rel in range(1, outer_count)]

    barrier = pltpu.get_barrier_semaphore()

    def greet(device):
        pl.semaphore_signal(barrier, inc=1, device_id=device, device_id_type=MESH)

    for peer in inner_peers:
        greet((o_me, peer))
    for peer in outer_peers:
        greet((peer, i_me))
    for rel in range(ranks):
        greet(at_rank(mate, rel)[0])

    for rel in range(ranks):
        greet(at_rank(lax.rem(other + blocks, blocks), rel)[0])
    pl.semaphore_wait(barrier, inner_count - 1 + outer_count - 1 + 2 * ranks)

    def remote(src, dst, send_sem, recv_sem, device):
        return pltpu.make_async_remote_copy(
            src_ref=src, dst_ref=dst, send_sem=send_sem, recv_sem=recv_sem,
            device_id=device, device_id_type=MESH,
        )

    def cols(index, width):
        return pl.ds(pl.multiple_of(index * width, LANES), width)

    own_copies = []
    for rel in range(1, ranks):
        device, target = at_rank(block, rel)
        slot = ranks - rel
        own_copies.append(remote(
            k_ref.at[:, cols(target, share)], own_k.at[slot],
            own_ss.at[0, slot], own_rs.at[0, slot], device))
        own_copies.append(remote(
            q_ref.at[:, cols(target, q_share)], q_all.at[slot],
            q_ss.at[slot], q_rs.at[slot], device))
        own_copies.append(remote(
            v_ref.at[:, cols(target, share)], own_v.at[slot],
            own_ss.at[1, slot], own_rs.at[1, slot], device))
    for copy in own_copies:
        copy.start()

    def block_copies(which, k_dst, v_dst, ss, rs):
        made = []
        for part, (src, dst) in enumerate(((k_ref, k_dst), (v_ref, v_dst))):
            for rel in range(ranks):
                device, target = at_rank(which, rel)
                slot = (ranks - rel) % ranks
                made.append(remote(
                    src.at[:, cols(target, share)], dst.at[slot],
                    ss.at[part, slot], rs.at[part, slot], device))
        return made

    mate_copies = block_copies(mate, mate_k, mate_v, mate_ss, mate_rs)
    for copy in mate_copies:
        copy.start()

    @pl.when(has_other)
    def _():
        for copy in block_copies(other, other_k, other_v, other_ss, other_rs):
            copy.start()

    def spread(pool_ref):
        rows = pool_ref.shape[0]
        pool = pool_ref[...]
        return jnp.concatenate(
            [jnp.broadcast_to(pool[:, n:n + 1], (rows, HD)) for n in range(2 * KVH)], axis=1)

    pf = spread(pf_ref)
    pc = spread(pc_ref)
    paired = jnp.concatenate([k_ref[...], v_ref[...]], axis=1).astype(F32)
    fine = jnp.sum(paired.reshape(fine_dev, FINE, 2 * kv_width) * pf[None], axis=1).astype(BF16)
    fine_wide = fine.astype(F32)
    coarse = jnp.sum(
        fine_wide.reshape(coarse_dev, RATIO, 2 * kv_width) * pc[None], axis=1).astype(BF16)
    padded = -(-coarse_dev // 8) * 8
    coarse_wide = coarse.astype(F32)
    if padded > coarse_dev:
        coarse_wide = jnp.concatenate(
            [coarse_wide, jnp.zeros((padded - coarse_dev, 2 * kv_width), F32)], axis=0)
    for n in range(ranks):
        k_cols = slice(n * share, (n + 1) * share)
        v_cols = slice(kv_width + n * share, kv_width + (n + 1) * share)
        fine_send[n] = jnp.concatenate([fine[:, k_cols], fine[:, v_cols]], axis=1)
        coarse_send[n] = jnp.concatenate([coarse_wide[:, k_cols], coarse_wide[:, v_cols]], axis=1)
    fine_all[i_me] = fine_send[rank]
    coarse_pad[i_me] = coarse_send[rank]

    group_copies = []
    for n, peer in enumerate(inner_peers):
        peer_rank = lax.rem(peer, ranks)
        group_copies.append(remote(
            coarse_send.at[peer_rank], coarse_pad.at[i_me],
            cg_ss.at[n], cg_rs.at[n], (o_me, peer)))
        group_copies.append(remote(
            fine_send.at[peer_rank], fine_all.at[i_me],
            fine_ss.at[n], fine_rs.at[n], (o_me, peer)))
    for copy in group_copies:
        copy.start()

    low = (lax.broadcasted_iota(jnp.int32, (1, LANES), 1) < HD).astype(F32).astype(BF16)
    high = (lax.broadcasted_iota(jnp.int32, (1, LANES), 1) >= HD).astype(F32).astype(BF16)

    def variants(k_raw, v_raw, k_out, v_out, rows):
        k_swap = pltpu.roll(k_raw.astype(F32), HD, 1).astype(BF16)
        v_swap = pltpu.roll(v_raw.astype(F32), HD, 1).astype(BF16)
        for n in range(kv_local):
            at_low = (k_raw, v_raw) if n == 0 else (k_swap, v_swap)
            at_high = (k_swap, v_swap) if n == 0 else (k_raw, v_raw)
            k_out[n, 0, rows, :] = at_low[0] * low
            k_out[n, 1, rows, :] = at_high[0] * high
            v_out[n, 0, rows, :] = at_low[1] * low + high
            v_out[n, 1, rows, :] = at_high[1] * high + low

    q_all[0] = q_ref[:, cols(rank, q_share)]
    variants(k_ref[:, cols(rank, share)], v_ref[:, cols(rank, share)], ka, va, slice(0, tok))
    for copy in own_copies:
        copy.wait_recv()
    for slot in range(1, ranks):
        variants(own_k[slot], own_v[slot], ka, va, slice(slot * tok, (slot + 1) * tok))

    def unit(part, tile, half, k_set, v_set, bias, first):
        n = tile // tiles_per_kv
        query = q_all[part, :, cols(tile, LANES)]
        scores = lax.dot_general(
            query, k_set[n, half], (((1,), (1,)), ((), ())), preferred_element_type=F32)
        if bias is not None:
            scores = scores + bias
        peak = jnp.max(scores, axis=1, keepdims=True)
        at = (part * tiles + tile) * 2 + half
        if not first:
            before = peaks[at][:, :1]
            peak = jnp.maximum(peak, before)
        weights = jnp.exp2((scores - peak) * factor).astype(BF16)
        blended = jnp.dot(weights, v_set[n, half], preferred_element_type=F32)
        if not first:
            blended = blended + sums[at] * jnp.exp2((before - peak) * factor)
        return at, peak, blended

    def stage(parts, k_set, v_set, first):
        def body(step, carry):
            part = step // tiles
            tile = lax.rem(step, tiles)
            done = [unit(part, tile, half, k_set, v_set, None, first) for half in range(2)]
            for at, peak, blended in done:
                peaks[at] = jnp.broadcast_to(peak, (tok, LANES))
                sums[at] = blended
            return carry
        lax.fori_loop(0, parts * tiles, body, 0)

    stage(ranks, ka, va, True)

    for copy in group_copies:
        copy.wait_recv()
    for n in range(inner_count):
        coarse_group[n * coarse_dev:(n + 1) * coarse_dev, :] = coarse_pad[n, 0:coarse_dev, :]
    coarse_all[o_me] = coarse_group[...]
    outer_copies = []
    for n, peer in enumerate(outer_peers):
        outer_copies.append(remote(
            coarse_group, coarse_all.at[o_me], co_ss.at[n], co_rs.at[n], (peer, i_me)))
    for copy in outer_copies:
        copy.start()

    for copy in mate_copies:
        copy.wait_recv()
    for slot in range(ranks):
        variants(mate_k[slot], mate_v[slot], kb, vb, slice(slot * tok, (slot + 1) * tok))
    stage(ranks, kb, vb, False)

    for copy in outer_copies:
        copy.wait_recv()
    fine_rows = fine_all[...].reshape(fine_amount, 2 * share)
    variants(fine_rows[:, :share], fine_rows[:, share:], kc, vc, slice(BLOCK, BLOCK + fine_amount))
    coarse_rows = coarse_all[...].reshape(coarse_amount, 2 * share).astype(BF16)
    variants(coarse_rows[:, :share], coarse_rows[:, share:], kc, vc,
             slice(BLOCK + fine_amount, BLOCK + fine_amount + coarse_amount))
    far = fine_amount + coarse_amount
    spot = lax.broadcasted_iota(jnp.int32, (1, far), 1)
    fine_pos = o_me * group_tok + spot * FINE
    coarse_pos = (spot - fine_amount) * COARSE
    position = jnp.where(spot < fine_amount, fine_pos, coarse_pos)
    distance = jnp.abs(lax.div(position, BLOCK) - block)
    outside = (spot < fine_amount) | (lax.div(position, group_tok) != o_me)
    bias_ref[:, BLOCK:] = jnp.where((distance > 1) & outside, 0.0, MASKED_SCORE)

    @pl.when(has_other)
    def _():
        for copy in block_copies(other, other_k, other_v, other_ss, other_rs):
            copy.wait_recv()
        for slot in range(ranks):
            variants(other_k[slot], other_v[slot], kc, vc, slice(slot * tok, (slot + 1) * tok))
        bias_ref[:, :BLOCK] = jnp.zeros((1, BLOCK), F32)

    @pl.when(jnp.logical_not(has_other))
    def _():
        zero = jnp.zeros((BLOCK, LANES), BF16)
        for n in range(kv_local):
            for half in range(2):
                kc[n, half, 0:BLOCK, :] = zero
                vc[n, half, 0:BLOCK, :] = zero
        bias_ref[:, :BLOCK] = jnp.full((1, BLOCK), MASKED_SCORE, F32)

    is_low = lax.broadcasted_iota(jnp.int32, (1, LANES), 1) < HD

    def finish(part, tile):
        bias = bias_ref[...]
        lower, upper = [unit(part, tile, half, kc, vc, bias, False)[2] for half in range(2)]
        totals = pltpu.roll(jnp.where(is_low, upper, lower), HD, 1)
        return jnp.where(is_low, lower, upper) / totals

    def att_copy(part, tile):
        device, _ = at_rank(block, part)
        slot = ranks - part - 1
        return remote(att_send.at[part - 1, tile], att_recv.at[slot, tile],
                      att_ss.at[slot, tile], att_rs.at[slot, tile], device)

    for part in range(1, ranks):
        def give(tile, carry):
            att_send[part - 1, tile] = finish(part, tile)
            att_copy(part, tile).start()
            return carry
        lax.fori_loop(0, tiles, give, 0)

    def keep(tile, square):
        attended = finish(0, tile)
        att_own[tile] = attended
        return square + attended * attended

    square = lax.fori_loop(0, tiles, keep, jnp.zeros((tok, LANES), F32))
    for part in range(1, ranks):
        for tile in range(tiles):
            att_copy(part, tile).wait_recv()
            attended = att_recv[ranks - part - 1, tile]
            square = square + attended * attended
    rescale = lax.rsqrt(jnp.sum(square, axis=1, keepdims=True) / (HQ * HD) + EPSILON)
    for slot in range(ranks):
        column = lax.rem(rank + slot, ranks) * tiles
        for tile in range(tiles):
            attended = att_own[tile] if slot == 0 else att_recv[slot - 1, tile]
            where = cols(column + tile, LANES)
            out_ref[:, where] = (attended * rescale * gain_ref[:, where]).astype(BF16)

    for copy in own_copies + mate_copies + group_copies + outer_copies:
        copy.wait_send()

    @pl.when(has_other)
    def _():
        for copy in block_copies(other, other_k, other_v, other_ss, other_rs):
            copy.wait_send()

    for part in range(1, ranks):
        for tile in range(tiles):
            att_copy(part, tile).wait_send()


def local(outer_count, inner_count, queries, keys, values, pool_fine, pool_coarse, gain):
    tok = queries.shape[0]
    ranks = BLOCK // tok
    share = KVH * HD // ranks
    kv_local = share // HD
    q_share = HQ * HD // ranks
    tiles = q_share // LANES
    group_tok = tok * inner_count
    far = group_tok // FINE + outer_count * group_tok // COARSE
    coarse_dev = tok // COARSE
    padded = -(-coarse_dev // 8) * 8
    assert ranks >= 2 and BLOCK % tok == 0 and kv_local == 2 and share == LANES
    assert inner_count % ranks == 0 and (outer_count * inner_count // ranks) % 2 == 0
    dma = pltpu.SemaphoreType.DMA
    vmem = pltpu.VMEM
    near = lambda: vmem((ranks, tok, share), BF16)
    sets = lambda amount: vmem((kv_local, 2, amount, LANES), BF16)
    units = ranks * tiles * 2
    pair = lambda: dma((2, ranks))
    return pl.pallas_call(
        functools.partial(kernel, outer_count, inner_count),
        out_shape=jax.ShapeDtypeStruct((tok, HQ * HD), BF16),
        in_specs=[pl.BlockSpec(memory_space=pltpu.VMEM)] * 6,
        out_specs=pl.BlockSpec(memory_space=pltpu.VMEM),
        scratch_shapes=[
            vmem((ranks, tok, q_share), BF16),
            near(), near(), near(), near(), near(), near(),
            sets(BLOCK), sets(BLOCK), sets(BLOCK), sets(BLOCK),
            sets(BLOCK + far), sets(BLOCK + far), vmem((1, BLOCK + far), F32),
            vmem((ranks, tok // FINE, 2 * share), BF16),
            vmem((inner_count, tok // FINE, 2 * share), BF16),
            vmem((ranks, padded, 2 * share), F32),
            vmem((inner_count, padded, 2 * share), F32),
            vmem((inner_count * coarse_dev, 2 * share), F32),
            vmem((outer_count, inner_count * coarse_dev, 2 * share), F32),
            vmem((units, tok, LANES), F32),
            vmem((units, tok, LANES), F32),
            vmem((tiles, tok, LANES), F32),
            vmem((ranks - 1, tiles, tok, LANES), F32),
            vmem((ranks - 1, tiles, tok, LANES), F32),
            dma((ranks,)), dma((ranks,)),
            pair(), pair(), pair(), pair(), pair(), pair(),
            dma((inner_count - 1,)), dma((inner_count - 1,)),
            dma((inner_count - 1,)), dma((inner_count - 1,)),
            dma((outer_count - 1,)), dma((outer_count - 1,)),
            dma((ranks - 1, tiles)), dma((ranks - 1, tiles)),
        ],
        compiler_params=pltpu.CompilerParams(
            collective_id=0, has_side_effects=True, vmem_limit_bytes=56 * 1024 * 1024),
    )(queries, keys, values, pool_fine, pool_coarse, gain.reshape(1, -1))


def solution(mesh):
    rows = P(("outer", "inner"), None)
    return jax.shard_map(
        functools.partial(local, mesh.shape["outer"], mesh.shape["inner"]),
        mesh=mesh, in_specs=(rows, rows, rows, P(), P(), P()),
        out_specs=rows, check_vma=False,
    )
```

time: 157 us -> 43 us (0.27)
  the two profiles are of different devices: /device:TPU:1 before, /device:TPU:3 now
where the time goes in v1:
time: 43 us; the launch traced here: 42.8 us
  Pallas kernels  39.6 us (92%)
  local copies, waits for them, and re-layouts  3.22 us (7%)
    pallas_call x1, Pallas kernels, local(): pl.pallas_call(functools.partial(kernel, outer_count, inner_count), out_s...  39.6 us
    unnamed x2, local copies, waits for them, and re-layouts  3.22 us

profile of v1, /device:TPU:3, one launch (start us, length us, event | category | flops | bytes accessed | tf_op | source)
XLA Modules:
  0.0 42.8 jit_solution(4474354712427441297)
XLA Ops:
  0.0 1.4 %copy.7.pf_ref = f32[16,8]{1,0:T(8,128)} copy(f32[16,8]{0,1:T(8,128)} %param.9) | data formatting | bytes 1024 | tf_op args[3]
  1.4 39.6 %shard_map.64 = bf16[256,1024]{1,0:T(8,128)(2,1)} custom-call(bf16[256,1024]{1,0:T(8,128)(2,1)} %q_ref.1, bf16[256,256]{1,0:T(8,128)(2,1)} %k_ref.1, bf16[256,256]{1,0:T(8,128)(2,1)} %v_ref.1, f32[16,8]{1,0:T(8,128)} %copy.7.pf_ref, f32[8,8]{1,0:T(8,128)} %pc_ref.1, f32[1,1024]{1,0:T(1,128)} %bitcast.1), custom_call_target="tpu_custom_call" | custom-call | tf_op jit(solution)/shard_map/pallas_call | solution.py:345
  40.9 1.9 %copy.9 = bf16[256,1024]{1,0:T(8,128)(2,1)} copy(bf16[256,1024]{1,0:T(8,128)(2,1)} %shard_map.64) | data formatting | bytes 1048576

commit v2 on v1

--- a/solution.py
+++ b/solution.py
@@ -26,11 +26,12 @@
 
 def kernel(
     outer_count, inner_count,
-    q_ref, k_ref, v_ref, pf_ref, pc_ref, gain_ref, out_ref,
+    q_hbm, k_hbm, v_hbm, pf_hbm, pc_hbm, out_ref,
+    q_ref, k_ref, v_ref, pf_ref, pc_ref, in_sems,
     q_all, own_k, own_v, mate_k, mate_v, other_k, other_v,
     ka, va, kb, vb, kc, vc, bias_ref,
     fine_send, fine_all, coarse_send, coarse_pad, coarse_group, coarse_all,
-    peaks, sums, att_own, att_send, att_recv,
+    peaks, sums, att_send, att_recv,
     q_ss, q_rs, own_ss, own_rs, mate_ss, mate_rs, other_ss, other_rs,
     fine_ss, fine_rs, cg_ss, cg_rs, co_ss, co_rs, att_ss, att_rs,
 ):
@@ -57,8 +58,10 @@
     rank = lax.rem(linear, ranks)
     odd = lax.rem(block, 2)
     mate = block + 1 - 2 * odd
-    other = block - 1 + 2 * odd
-    has_other = (other >= 0) & (other < blocks)
+    relay_from = block - 2 + 4 * odd
+    relay_to = block + 2 - 4 * odd
+    has_other = (relay_from >= 0) & (relay_from < blocks)
+    has_next = (relay_to >= 0) & (relay_to < blocks)
 
     def at_rank(which_block, rel):
         target_rank = lax.rem(rank + rel, ranks)
@@ -67,6 +70,14 @@
 
     inner_peers = [lax.rem(i_me + rel, inner_count) for rel in range(1, inner_count)]
     outer_peers = [lax.rem(o_me + rel, outer_count) for rel in range(1, outer_count)]
+
+    loads = [
+        pltpu.make_async_copy(src, dst, in_sems.at[n])
+        for n, (src, dst) in enumerate((
+            (k_hbm, k_ref), (q_hbm, q_ref), (v_hbm, v_ref), (pf_hbm, pf_ref), (pc_hbm, pc_ref)))
+    ]
+    for load in loads:
+        load.start()
 
     barrier = pltpu.get_barrier_semaphore()
 
@@ -80,9 +91,12 @@
     for rel in range(ranks):
         greet(at_rank(mate, rel)[0])
 
-    for rel in range(ranks):
-        greet(at_rank(lax.rem(other + blocks, blocks), rel)[0])
-    pl.semaphore_wait(barrier, inner_count - 1 + outer_count - 1 + 2 * ranks)
+    for which in (relay_from, relay_to):
+        greet(at_rank(lax.rem(which + blocks, blocks), 0)[0])
+    pl.semaphore_wait(barrier, inner_count - 1 + outer_count - 1 + ranks + 2)
+
+    for load in loads:
+        load.wait()
 
     def remote(src, dst, send_sem, recv_sem, device):
         return pltpu.make_async_remote_copy(
@@ -109,34 +123,34 @@
     for copy in own_copies:
         copy.start()
 
-    def block_copies(which, k_dst, v_dst, ss, rs):
+    def mate_copies_of(part, src, dst):
         made = []
-        for part, (src, dst) in enumerate(((k_ref, k_dst), (v_ref, v_dst))):
-            for rel in range(ranks):
-                device, target = at_rank(which, rel)
-                slot = (ranks - rel) % ranks
-                made.append(remote(
-                    src.at[:, cols(target, share)], dst.at[slot],
-                    ss.at[part, slot], rs.at[part, slot], device))
+        for rel in range(ranks):
+            device, target = at_rank(mate, rel)
+            slot = (ranks - rel) % ranks
+            made.append(remote(
+                src.at[:, cols(target, share)], dst.at[slot],
+                mate_ss.at[part, slot], mate_rs.at[part, slot], device))
         return made
 
-    mate_copies = block_copies(mate, mate_k, mate_v, mate_ss, mate_rs)
-    for copy in mate_copies:
+    def relay_copies(part):
+        device = at_rank(relay_to, 0)[0]
+        src, dst = ((mate_k, other_k), (mate_v, other_v))[part]
+        return [remote(src.at[slot], dst.at[slot], other_ss.at[part, slot],
+                       other_rs.at[part, slot], device) for slot in range(ranks)]
+
+    mate_k_copies = mate_copies_of(0, k_ref, mate_k)
+    mate_v_copies = mate_copies_of(1, v_ref, mate_v)
+    for copy in mate_k_copies:
         copy.start()
 
-    @pl.when(has_other)
-    def _():
-        for copy in block_copies(other, other_k, other_v, other_ss, other_rs):
-            copy.start()
-
-    def spread(pool_ref):
-        rows = pool_ref.shape[0]
-        pool = pool_ref[...]
+    def spread(pool):
+        rows = pool.shape[0]
         return jnp.concatenate(
             [jnp.broadcast_to(pool[:, n:n + 1], (rows, HD)) for n in range(2 * KVH)], axis=1)
 
-    pf = spread(pf_ref)
-    pc = spread(pc_ref)
+    pf = spread(pf_ref[...].T)
+    pc = spread(pc_ref[...])
     paired = jnp.concatenate([k_ref[...], v_ref[...]], axis=1).astype(F32)
     fine = jnp.sum(paired.reshape(fine_dev, FINE, 2 * kv_width) * pf[None], axis=1).astype(BF16)
     fine_wide = fine.astype(F32)
@@ -164,7 +178,7 @@
         group_copies.append(remote(
             fine_send.at[peer_rank], fine_all.at[i_me],
             fine_ss.at[n], fine_rs.at[n], (o_me, peer)))
-    for copy in group_copies:
+    for copy in group_copies + mate_v_copies:
         copy.start()
 
     low = (lax.broadcasted_iota(jnp.int32, (1, LANES), 1) < HD).astype(F32).astype(BF16)
@@ -197,10 +211,12 @@
             scores = scores + bias
         peak = jnp.max(scores, axis=1, keepdims=True)
         at = (part * tiles + tile) * 2 + half
+        peak = jnp.broadcast_to(peak, (tok, LANES))
         if not first:
-            before = peaks[at][:, :1]
+            before = peaks[at]
             peak = jnp.maximum(peak, before)
-        weights = jnp.exp2((scores - peak) * factor).astype(BF16)
+        wide = jnp.concatenate([peak] * (scores.shape[1] // LANES), axis=1)
+        weights = jnp.exp2((scores - wide) * factor).astype(BF16)
         blended = jnp.dot(weights, v_set[n, half], preferred_element_type=F32)
         if not first:
             blended = blended + sums[at] * jnp.exp2((before - peak) * factor)
@@ -212,7 +228,7 @@
             tile = lax.rem(step, tiles)
             done = [unit(part, tile, half, k_set, v_set, None, first) for half in range(2)]
             for at, peak, blended in done:
-                peaks[at] = jnp.broadcast_to(peak, (tok, LANES))
+                peaks[at] = peak
                 sums[at] = blended
             return carry
         lax.fori_loop(0, parts * tiles, body, 0)
@@ -231,8 +247,14 @@
     for copy in outer_copies:
         copy.start()
 
-    for copy in mate_copies:
-        copy.wait_recv()
+    for part, copies in enumerate((mate_k_copies, mate_v_copies)):
+        for copy in copies:
+            copy.wait_recv()
+
+        @pl.when(has_next)
+        def _():
+            for copy in relay_copies(part):
+                copy.start()
     for slot in range(ranks):
         variants(mate_k[slot], mate_v[slot], kb, vb, slice(slot * tok, (slot + 1) * tok))
     stage(ranks, kb, vb, False)
@@ -255,7 +277,7 @@
 
     @pl.when(has_other)
     def _():
-        for copy in block_copies(other, other_k, other_v, other_ss, other_rs):
+        for copy in relay_copies(0) + relay_copies(1):
             copy.wait_recv()
         for slot in range(ranks):
             variants(other_k[slot], other_v[slot], kc, vc, slice(slot * tok, (slot + 1) * tok))
@@ -291,36 +313,35 @@
             return carry
         lax.fori_loop(0, tiles, give, 0)
 
-    def keep(tile, square):
-        attended = finish(0, tile)
-        att_own[tile] = attended
-        return square + attended * attended
-
-    square = lax.fori_loop(0, tiles, keep, jnp.zeros((tok, LANES), F32))
+    def keep(tile, carry):
+        out_ref[:, cols(rank * tiles + tile, LANES)] = finish(0, tile)
+        return carry
+
+    lax.fori_loop(0, tiles, keep, 0)
     for part in range(1, ranks):
+        slot = ranks - part
+        column = lax.rem(rank + slot, ranks) * tiles
         for tile in range(tiles):
             att_copy(part, tile).wait_recv()
-            attended = att_recv[ranks - part - 1, tile]
-            square = square + attended * attended
-    rescale = lax.rsqrt(jnp.sum(square, axis=1, keepdims=True) / (HQ * HD) + EPSILON)
-    for slot in range(ranks):
-        column = lax.rem(rank + slot, ranks) * tiles
-        for tile in range(tiles):
-            attended = att_own[tile] if slot == 0 else att_recv[slot - 1, tile]
-            where = cols(column + tile, LANES)
-            out_ref[:, where] = (attended * rescale * gain_ref[:, where]).astype(BF16)
-
-    for copy in own_copies + mate_copies + group_copies + outer_copies:
+            out_ref[:, cols(column + tile, LANES)] = att_recv[slot - 1, tile]
+
+    for copy in own_copies + mate_k_copies + mate_v_copies + group_copies + outer_copies:
         copy.wait_send()
 
-    @pl.when(has_other)
+    @pl.when(has_next)
     def _():
-        for copy in block_copies(other, other_k, other_v, other_ss, other_rs):
+        for copy in relay_copies(0) + relay_copies(1):
             copy.wait_send()
 
     for part in range(1, ranks):
         for tile in range(tiles):
             att_copy(part, tile).wait_send()
+
+
+def norm_kernel(attended_ref, gain_ref, out_ref):
+    attended = attended_ref[...]
+    rescale = lax.rsqrt(jnp.mean(attended * attended, axis=1, keepdims=True) + EPSILON)
+    out_ref[...] = (attended * rescale * gain_ref[...]).astype(BF16)
 
 
 def local(outer_count, inner_count, queries, keys, values, pool_fine, pool_coarse, gain):
@@ -342,12 +363,14 @@
     sets = lambda amount: vmem((kv_local, 2, amount, LANES), BF16)
     units = ranks * tiles * 2
     pair = lambda: dma((2, ranks))
-    return pl.pallas_call(
+    attended = pl.pallas_call(
         functools.partial(kernel, outer_count, inner_count),
-        out_shape=jax.ShapeDtypeStruct((tok, HQ * HD), BF16),
-        in_specs=[pl.BlockSpec(memory_space=pltpu.VMEM)] * 6,
+        out_shape=jax.ShapeDtypeStruct((tok, HQ * HD), F32),
+        in_specs=[pl.BlockSpec(memory_space=pltpu.HBM)] * 5,
         out_specs=pl.BlockSpec(memory_space=pltpu.VMEM),
         scratch_shapes=[
+            vmem(queries.shape, BF16), vmem(keys.shape, BF16), vmem(values.shape, BF16),
+            vmem(pool_fine.shape[::-1], F32), vmem(pool_coarse.shape, F32), dma((5,)),
             vmem((ranks, tok, q_share), BF16),
             near(), near(), near(), near(), near(), near(),
             sets(BLOCK), sets(BLOCK), sets(BLOCK), sets(BLOCK),
@@ -360,7 +383,6 @@
             vmem((outer_count, inner_count * coarse_dev, 2 * share), F32),
             vmem((units, tok, LANES), F32),
             vmem((units, tok, LANES), F32),
-            vmem((tiles, tok, LANES), F32),
             vmem((ranks - 1, tiles, tok, LANES), F32),
             vmem((ranks - 1, tiles, tok, LANES), F32),
             dma((ranks,)), dma((ranks,)),
@@ -371,8 +393,16 @@
             dma((ranks - 1, tiles)), dma((ranks - 1, tiles)),
         ],
         compiler_params=pltpu.CompilerParams(
-            collective_id=0, has_side_effects=True, vmem_limit_bytes=56 * 1024 * 1024),
-    )(queries, keys, values, pool_fine, pool_coarse, gain.reshape(1, -1))
+            collective_id=0, has_side_effects=True, vmem_limit_bytes=32 * 1024 * 1024),
+    )(*(pltpu.with_memory_space_constraint(array, pltpu.HBM) for array in (
+        queries, keys, values, pool_fine.T, pool_coarse)))
+    return pl.pallas_call(
+        norm_kernel,
+        out_shape=jax.ShapeDtypeStruct((tok, HQ * HD), BF16),
+        in_specs=[pl.BlockSpec(memory_space=pltpu.VMEM)] * 2,
+        out_specs=pl.BlockSpec(memory_space=pltpu.VMEM),
+        compiler_params=pltpu.CompilerParams(vmem_limit_bytes=8 * 1024 * 1024),
+    )(attended, gain.reshape(1, -1))
 
 
 def solution(mesh):

time: 43 us -> 31.1 us (0.72)
  the two profiles are of different devices: /device:TPU:3 before, /device:TPU:1 now
where the time goes in v2:
time: 31.1 us; the launch traced here: 30.7 us
  Pallas kernels  30.6 us (98%)
    pallas_call x1, Pallas kernels, local(): pl.pallas_call(functools.partial(kernel, outer_count, inner_count), out_s...  29.6 us
    pallas_call x1, Pallas kernels, local(): pl.pallas_call(norm_kernel, out_shape=jax.ShapeDtypeStruct((tok, HQ * HD)...  0.99 us

profile of v2, /device:TPU:1, one launch (start us, length us, event | category | flops | bytes accessed | tf_op | source)
XLA Modules:
  0.0 30.7 jit_solution(11999510672178337909)
XLA Ops:
  0.0 0.0 copy-start
  0.0 29.6 %shard_map.64.attended_ref = f32[256,1024]{1,0:T(8,128)S(1)} custom-call(bf16[256,1024]{1,0:T(8,128)(2,1)} %q_hbm.1, bf16[256,256]{1,0:T(8,128)(2,1)} %k_hbm.1, bf16[256,256]{1,0:T(8,128)(2,1)} %v_hbm.1, f32[8,16]{1,0:T(8,128)} %bitcast.3, f32[8,8]{1,0:T(8,128)} %pc_hbm.1), custom_call_target="tpu_custom_call" | custom-call | tf_op jit(solution)/shard_map/pallas_call | solution.py:366
  29.7 0.0 copy-done
  29.7 1.0 %shard_map.65 = bf16[256,1024]{1,0:T(8,128)(2,1)} custom-call(f32[256,1024]{1,0:T(8,128)S(1)} %shard_map.64.attended_ref, f32[1,1024]{1,0:T(1,128)S(1)} %bitcast.2), custom_call_target="tpu_custom_call" | custom-call | tf_op jit(solution)/shard_map/pallas_call | solution.py:399
Async XLA Ops:
  0.0 29.7 %copy-start = (f32[1024]{0:T(1024)S(1)}, f32[1024]{0:T(1024)}, u32[]{:S(2)}) copy-start(f32[1024]{0:T(1024)} %param.11) | copy-start | bytes 12292

commit v3 on v2

--- a/solution.py
+++ b/solution.py
@@ -43,6 +43,7 @@
     tiles = q_share // LANES
     kv_local = share // HD
     tiles_per_kv = tiles // kv_local
+    rows_kv = tiles_per_kv * tok
     fine_dev = tok // FINE
     coarse_dev = tok // COARSE
     group_tok = tok * inner_count
@@ -93,7 +94,6 @@
 
     for which in (relay_from, relay_to):
         greet(at_rank(lax.rem(which + blocks, blocks), 0)[0])
-    pl.semaphore_wait(barrier, inner_count - 1 + outer_count - 1 + ranks + 2)
 
     for load in loads:
         load.wait()
@@ -120,8 +120,6 @@
         own_copies.append(remote(
             v_ref.at[:, cols(target, share)], own_v.at[slot],
             own_ss.at[1, slot], own_rs.at[1, slot], device))
-    for copy in own_copies:
-        copy.start()
 
     def mate_copies_of(part, src, dst):
         made = []
@@ -141,8 +139,6 @@
 
     mate_k_copies = mate_copies_of(0, k_ref, mate_k)
     mate_v_copies = mate_copies_of(1, v_ref, mate_v)
-    for copy in mate_k_copies:
-        copy.start()
 
     def spread(pool):
         rows = pool.shape[0]
@@ -178,8 +174,6 @@
         group_copies.append(remote(
             fine_send.at[peer_rank], fine_all.at[i_me],
             fine_ss.at[n], fine_rs.at[n], (o_me, peer)))
-    for copy in group_copies + mate_v_copies:
-        copy.start()
 
     low = (lax.broadcasted_iota(jnp.int32, (1, LANES), 1) < HD).astype(F32).astype(BF16)
     high = (lax.broadcasted_iota(jnp.int32, (1, LANES), 1) >= HD).astype(F32).astype(BF16)
@@ -195,45 +189,54 @@
             v_out[n, 0, rows, :] = at_low[1] * low + high
             v_out[n, 1, rows, :] = at_high[1] * high + low
 
-    q_all[0] = q_ref[:, cols(rank, q_share)]
-    variants(k_ref[:, cols(rank, share)], v_ref[:, cols(rank, share)], ka, va, slice(0, tok))
-    for copy in own_copies:
-        copy.wait_recv()
-    for slot in range(1, ranks):
-        variants(own_k[slot], own_v[slot], ka, va, slice(slot * tok, (slot + 1) * tok))
-
-    def unit(part, tile, half, k_set, v_set, bias, first):
-        n = tile // tiles_per_kv
-        query = q_all[part, :, cols(tile, LANES)]
+    def unit(part, n, half, k_set, v_set, span, bias, first):
+        query = jnp.concatenate(
+            [q_all[part, :, cols(n * tiles_per_kv + x, LANES)] for x in range(tiles_per_kv)],
+            axis=0)
         scores = lax.dot_general(
-            query, k_set[n, half], (((1,), (1,)), ((), ())), preferred_element_type=F32)
+            query, k_set[n, half, span, :], (((1,), (1,)), ((), ())),
+            preferred_element_type=F32)
         if bias is not None:
             scores = scores + bias
-        peak = jnp.max(scores, axis=1, keepdims=True)
-        at = (part * tiles + tile) * 2 + half
-        peak = jnp.broadcast_to(peak, (tok, LANES))
+        peak = jnp.broadcast_to(jnp.max(scores, axis=1, keepdims=True), (rows_kv, LANES))
+        at = (part * kv_local + n) * 2 + half
         if not first:
             before = peaks[at]
             peak = jnp.maximum(peak, before)
         wide = jnp.concatenate([peak] * (scores.shape[1] // LANES), axis=1)
         weights = jnp.exp2((scores - wide) * factor).astype(BF16)
-        blended = jnp.dot(weights, v_set[n, half], preferred_element_type=F32)
+        blended = jnp.dot(weights, v_set[n, half, span, :], preferred_element_type=F32)
         if not first:
             blended = blended + sums[at] * jnp.exp2((before - peak) * factor)
         return at, peak, blended
 
-    def stage(parts, k_set, v_set, first):
+    def stage(start, stop, k_set, v_set, span, first):
         def body(step, carry):
-            part = step // tiles
-            tile = lax.rem(step, tiles)
-            done = [unit(part, tile, half, k_set, v_set, None, first) for half in range(2)]
-            for at, peak, blended in done:
+            part = start + step // kv_local
+            n = lax.rem(step, kv_local)
+            for at, peak, blended in [
+                unit(part, n, half, k_set, v_set, span, None, first) for half in range(2)
+            ]:
                 peaks[at] = peak
                 sums[at] = blended
             return carry
-        lax.fori_loop(0, parts * tiles, body, 0)
-
-    stage(ranks, ka, va, True)
+        lax.fori_loop(0, (stop - start) * kv_local, body, 0)
+
+    q_all[0] = q_ref[:, cols(rank, q_share)]
+    variants(k_ref[:, cols(rank, share)], v_ref[:, cols(rank, share)], ka, va, slice(0, tok))
+    stage(0, 1, ka, va, slice(0, tok), True)
+
+    pl.semaphore_wait(barrier, inner_count - 1 + outer_count - 1 + ranks + 2)
+    for copy in own_copies + mate_k_copies + group_copies + mate_v_copies:
+        copy.start()
+
+    for copy in own_copies:
+        copy.wait_recv()
+    for slot in range(1, ranks):
+        variants(own_k[slot], own_v[slot], ka, va, slice(slot * tok, (slot + 1) * tok))
+        variants(own_k[slot], own_v[slot], kb, vb, slice((slot - 1) * tok, slot * tok))
+
+    stage(1, ranks, ka, va, slice(0, BLOCK), True)
 
     for copy in group_copies:
         copy.wait_recv()
@@ -256,8 +259,10 @@
             for copy in relay_copies(part):
                 copy.start()
     for slot in range(ranks):
-        variants(mate_k[slot], mate_v[slot], kb, vb, slice(slot * tok, (slot + 1) * tok))
-    stage(ranks, kb, vb, False)
+        variants(mate_k[slot], mate_v[slot], kb, vb,
+                 slice(BLOCK + (slot - 1) * tok, BLOCK + slot * tok))
+    stage(0, 1, kb, vb, slice(0, 2 * BLOCK - tok), False)
+    stage(1, ranks, kb, vb, slice(BLOCK - tok, 2 * BLOCK - tok), False)
 
     for copy in outer_copies:
         copy.wait_recv()
@@ -294,9 +299,9 @@
 
     is_low = lax.broadcasted_iota(jnp.int32, (1, LANES), 1) < HD
 
-    def finish(part, tile):
-        bias = bias_ref[...]
-        lower, upper = [unit(part, tile, half, kc, vc, bias, False)[2] for half in range(2)]
+    def finish(part, n):
+        lower, upper = [
+            unit(part, n, half, kc, vc, slice(None), bias_ref[...], False)[2] for half in range(2)]
         totals = pltpu.roll(jnp.where(is_low, upper, lower), HD, 1)
         return jnp.where(is_low, lower, upper) / totals
 
@@ -307,17 +312,23 @@
                       att_ss.at[slot, tile], att_rs.at[slot, tile], device)
 
     for part in range(1, ranks):
-        def give(tile, carry):
-            att_send[part - 1, tile] = finish(part, tile)
-            att_copy(part, tile).start()
+        def give(n, carry):
+            attended = finish(part, n)
+            for x in range(tiles_per_kv):
+                tile = n * tiles_per_kv + x
+                att_send[part - 1, tile] = attended[x * tok:(x + 1) * tok]
+                att_copy(part, tile).start()
             return carry
-        lax.fori_loop(0, tiles, give, 0)
-
-    def keep(tile, carry):
-        out_ref[:, cols(rank * tiles + tile, LANES)] = finish(0, tile)
+        lax.fori_loop(0, kv_local, give, 0)
+
+    def keep(n, carry):
+        attended = finish(0, n)
+        for x in range(tiles_per_kv):
+            tile = n * tiles_per_kv + x
+            out_ref[:, cols(rank * tiles + tile, LANES)] = attended[x * tok:(x + 1) * tok]
         return carry
 
-    lax.fori_loop(0, tiles, keep, 0)
+    lax.fori_loop(0, kv_local, keep, 0)
     for part in range(1, ranks):
         slot = ranks - part
         column = lax.rem(rank + slot, ranks) * tiles
@@ -361,7 +372,8 @@
     vmem = pltpu.VMEM
     near = lambda: vmem((ranks, tok, share), BF16)
     sets = lambda amount: vmem((kv_local, 2, amount, LANES), BF16)
-    units = ranks * tiles * 2
+    units = ranks * kv_local * 2
+    rows_kv = tiles // kv_local * tok
     pair = lambda: dma((2, ranks))
     attended = pl.pallas_call(
         functools.partial(kernel, outer_count, inner_count),
@@ -373,7 +385,7 @@
             vmem(pool_fine.shape[::-1], F32), vmem(pool_coarse.shape, F32), dma((5,)),
             vmem((ranks, tok, q_share), BF16),
             near(), near(), near(), near(), near(), near(),
-            sets(BLOCK), sets(BLOCK), sets(BLOCK), sets(BLOCK),
+            sets(BLOCK), sets(BLOCK), sets(2 * BLOCK - tok), sets(2 * BLOCK - tok),
             sets(BLOCK + far), sets(BLOCK + far), vmem((1, BLOCK + far), F32),
             vmem((ranks, tok // FINE, 2 * share), BF16),
             vmem((inner_count, tok // FINE, 2 * share), BF16),
@@ -381,8 +393,8 @@
             vmem((inner_count, padded, 2 * share), F32),
             vmem((inner_count * coarse_dev, 2 * share), F32),
             vmem((outer_count, inner_count * coarse_dev, 2 * share), F32),
-            vmem((units, tok, LANES), F32),
-            vmem((units, tok, LANES), F32),
+            vmem((units, rows_kv, LANES), F32),
+            vmem((units, rows_kv, LANES), F32),
             vmem((ranks - 1, tiles, tok, LANES), F32),
             vmem((ranks - 1, tiles, tok, LANES), F32),
             dma((ranks,)), dma((ranks,)),

time: 31.1 us -> 27.8 us (0.89)
  Pallas kernels: 30.6 us -> 27.6 us
    pallas_call x1, Pallas kernels: 29.6 us -> 26.6 us  [local(): pl.pallas_call(functools.partial(kernel, outer_count, inner_count), out_s...]
where the time goes in v3:
time: 27.8 us; the launch traced here: 27.6 us
  Pallas kernels  27.6 us (99%)
    pallas_call x1, Pallas kernels, local(): pl.pallas_call(functools.partial(kernel, outer_count, inner_count), out_s...  26.6 us
    pallas_call x1, Pallas kernels, local(): pl.pallas_call(norm_kernel, out_shape=jax.ShapeDtypeStruct((tok, HQ * HD)...  0.99 us

profile of v3, /device:TPU:1, one launch (start us, length us, event | category | flops | bytes accessed | tf_op | source)
XLA Modules:
  0.0 27.6 jit_solution(6863229593478810221)
XLA Ops:
  0.0 0.0 copy-start
  0.0 26.6 %shard_map.64.attended_ref = f32[256,1024]{1,0:T(8,128)S(1)} custom-call(bf16[256,1024]{1,0:T(8,128)(2,1)} %q_hbm.1, bf16[256,256]{1,0:T(8,128)(2,1)} %k_hbm.1, bf16[256,256]{1,0:T(8,128)(2,1)} %v_hbm.1, f32[8,16]{1,0:T(8,128)} %bitcast.3, f32[8,8]{1,0:T(8,128)} %pc_hbm.1), custom_call_target="tpu_custom_call" | custom-call | tf_op jit(solution)/shard_map/pallas_call | solution.py:378
  26.6 0.0 copy-done
  26.6 1.0 %shard_map.65 = bf16[256,1024]{1,0:T(8,128)(2,1)} custom-call(f32[256,1024]{1,0:T(8,128)S(1)} %shard_map.64.attended_ref, f32[1,1024]{1,0:T(1,128)S(1)} %bitcast.2), custom_call_target="tpu_custom_call" | custom-call | tf_op jit(solution)/shard_map/pallas_call | solution.py:411
Async XLA Ops:
  0.0 26.6 %copy-start = (f32[1024]{0:T(1024)S(1)}, f32[1024]{0:T(1024)}, u32[]{:S(2)}) copy-start(f32[1024]{0:T(1024)} %param.11) | copy-start | bytes 12292
